TPU v7x, 256 devices: a whole 4x4x8 slice. The times are simulated.
256 devices in a mesh: dp: 64 (over x, z_lo, y), expert: 4 (over z_hi, core).
Axes of the slice: x: 4, y: 4, z: 8 (z_hi: 2, z_lo: 4; z = z_hi * 4 + z_lo), core: 2. Of those that a mesh axis runs over, the one named last changes fastest.
Arguments:
- master: float32 [4, 7168, 2048], P('expert', 'dp'), may hold values from -6 to 6
- first_moment: float32 [4, 7168, 2048], P('expert', 'dp'), may hold values from -0.06 to 0.06
- second_moment: float32 [4, 7168, 2048], P('expert', 'dp'), may hold values from 1e-05 to 0.001
- rotation: int32 [4, 64, 1], replicated, may hold values from 0 to 63; in each aligned block of 64 rows (0 to 63, 64 to 127, ..., all dimensions but the last counted through in order) at most 3 rows name the same one
- assignment: int32 [256], replicated, may hold values from 0 to 255, each once
Outputs:
- saved_master: float32 [4, 256, 3, 448, 128], P('expert', 'dp')
- saved_update: float32 [4, 256, 3, 448, 128], P('expert', 'dp')
- checksums: float32 [4, 2, 256], replicated
Inputs may be any that keep to these rules, and one draw needn't show every extreme that they name: rotation[r, j, 0] is the dp index that writes span j of round r; within one round no index is named more than 3 times, and in some round one index is named exactly 3 times. `assignment`: a permutation of the spans' checksum slots.
All inputs are finite; a program needn't handle non-finite values.
Results may differ from a plain program's by a relative error of at most 0.00002.
Values sent between devices are 32-bit elements; how exact they have to be, the bound alone decides.
A program may use at most 64 MiB of HBM per device.

v0:
```python
import math
import jax
import jax.numpy as jnp
from jax import lax
from jax.sharding import Mesh
from jax.sharding import PartitionSpec as P

LANE = 128
MOST = 3
STEP = 20
DP = ("dp_0", "dp_1", "dp_2")
EXPERT = ("expert_0", "expert_1")
DP_EXPERT = ("dp_0", "dp_1", "dp_2", "expert_0", "expert_1")
BETA_ONE = 0.9
BETA_TWO = 0.95
EPSILON = 1e-08


def sent_together(arrays, axis, split_dim, concat_dim, along):
    ends, at = ([], 0)
    for a in arrays[:-1]:
        at += a.shape[along]
        ends.append(at)
    both = jnp.concatenate(arrays, axis=along)
    return tuple(
        jnp.split(
            lax.all_to_all(both, axis, split_axis=split_dim, concat_axis=concat_dim, tiled=True),
            ends,
            axis=along,
        )
    )


def one_axis_at_a_time(array, axes):
    for axis in axes:
        array = lax.psum(array, axis)
    return array


def scaled_moment(first_part, second_part):
    corr_one = 1.0 - BETA_ONE**STEP
    corr_two = 1.0 - BETA_TWO**STEP
    return first_part / corr_one / (jnp.sqrt(second_part / corr_two) + EPSILON)


def slot_table(rotation, dp_count, most_slots):
    owners = rotation[:, :, 0]
    span_ids = jnp.arange(dp_count, dtype=jnp.int32)
    same_writer = owners[:, :, None] == owners[:, None, :]
    before = span_ids[None, :] < span_ids[:, None]
    slot_rank = jnp.sum((same_writer & before[None]).astype(jnp.int32), axis=2)
    writers = jnp.arange(dp_count, dtype=jnp.int32)
    slot_ids = jnp.arange(most_slots, dtype=jnp.int32)
    matches = (owners[:, None, None, :] == writers[None, None, :, None]) & (
        slot_rank[:, None, None, :] == slot_ids[None, :, None, None]
    )
    matches = matches.astype(jnp.int32)
    found_any = jnp.sum(matches, axis=3)
    picked = jnp.sum(matches * span_ids, axis=3)
    return picked + (1 - found_any) * dp_count


def position_weights(line_ids, per_row, lane_count):
    row_ids = line_ids // per_row
    col_ids = line_ids % per_row * lane_count
    lane_ids = jnp.arange(lane_count, dtype=jnp.int32)
    pattern = (row_ids[..., None] * 5 + (col_ids[..., None] + lane_ids) * 3) % 11
    return 1.0 + pattern.astype(jnp.float32) / 10.0


def deliver_slots(send_parts):
    return sent_together((send_parts[0], send_parts[1]), DP, 1, 1, 0)


def shards(master, first_moment, second_moment, rotation, assignment):
    dp_count = lax.axis_size(DP)
    group_count = lax.axis_size(EXPERT)
    position = lax.axis_index(DP)
    group_id = lax.axis_index(EXPERT)
    round_count = rotation.shape[0]
    rows_here = master.shape[1]
    lane_count = LANE
    per_row = master.shape[2] // lane_count
    lines_device = rows_here * per_row
    piece_len = lines_device // (round_count * dp_count)
    inv_count = 1.0 / math.sqrt(dp_count * piece_len * lane_count)
    table = slot_table(rotation, dp_count, MOST)
    round_ids = jnp.arange(round_count, dtype=jnp.int32)[:, None, None]

    def line_pieces(field_in):
        return field_in.reshape(round_count, dp_count, piece_len, lane_count)

    def padded_pieces(line_view):
        return jnp.concatenate(
            [line_view, jnp.zeros((round_count, 1, piece_len, lane_count), line_view.dtype)], axis=1
        )

    update = scaled_moment(first_moment, second_moment)
    master_lines = line_pieces(master)
    update_lines = line_pieces(update)
    local_lines = position * lines_device + jnp.arange(lines_device, dtype=jnp.int32).reshape(
        round_count, dp_count, piece_len
    )
    weights = position_weights(local_lines, per_row, lane_count)
    master_sums = (
        jnp.sum(master_lines * weights, axis=(2, 3)).reshape(round_count * dp_count) * inv_count
    )
    update_sums = (
        jnp.sum(update_lines * weights, axis=(2, 3)).reshape(round_count * dp_count) * inv_count
    )
    sources = (padded_pieces(master_lines), padded_pieces(update_lines))
    send_parts = tuple(
        (
            source[round_ids, table].reshape(round_count * MOST, dp_count, piece_len, lane_count)
            for source in sources
        )
    )
    delivered = deliver_slots(send_parts)
    saved_master = delivered[0].reshape(round_count, MOST, dp_count, piece_len, lane_count)
    saved_update = delivered[1].reshape(round_count, MOST, dp_count, piece_len, lane_count)
    span_count = assignment.shape[0]
    slot_ids = jnp.arange(span_count, dtype=jnp.int32)
    permuting = (assignment[:, None] == slot_ids[None, :]).astype(jnp.float32)
    both_sums = jnp.stack([master_sums, update_sums])
    placed_sums = jnp.sum(both_sums[:, :, None] * permuting[None], axis=1)
    in_slot = (jnp.arange(group_count, dtype=jnp.int32) == group_id).astype(jnp.float32)
    contribution = in_slot[:, None, None] * placed_sums[None]
    checksums = one_axis_at_a_time(contribution, DP_EXPERT)
    shape_out = (1, round_count, MOST, dp_count * piece_len, lane_count)
    return (saved_master.reshape(shape_out), saved_update.reshape(shape_out), checksums)


def solution(mesh):
    torus = Mesh(
        mesh.devices.reshape(4, 4, 4, 2, 2), ("dp_0", "dp_1", "dp_2", "expert_0", "expert_1")
    )
    in_specs = (P(EXPERT, DP, None), P(EXPERT, DP, None), P(EXPERT, DP, None), P(), P())
    out_specs = (P(EXPERT, DP, None, None, None), P(EXPERT, DP, None, None, None), P())
    return jax.shard_map(
        shards, mesh=torus, in_specs=in_specs, out_specs=out_specs, check_vma=False
    )
```

profile of v0, /device:TPU:71, one launch (start us, length us, event | category | flops | bytes accessed | tf_op | source)
XLA Modules:
  0.0 217.4 jit_solution(6803758860566984017)
XLA Ops:
  0.7 0.8 iota_compare_fusion.1
  1.4 1.0 convert_reduce_fusion
  2.4 0.5 fusion.7
  3.0 0.1 reshape.229
  3.1 1.8 add_divide_fusion
  4.9 0.2 reshape.221
  5.1 1.2 reshape.219
  6.3 0.1 concatenate.15
  6.3 1.3 concatenate.13
  7.6 6.6 %gather_fusion = f32[768,7,128]{2,1,0:T(8,128)} fusion(f32[4,65,7,128]{3,2,1,0:T(8,128)S(1)} %concatenate.13, s32[768]{0:T(1024)S(1)} %reshape.229), kind=kCustom, calls=%fused_computation | custom fusion | bytes 5511168 | tf_op jit(solution)/shard_map/gather | solution.py:114
  14.3 5.3 %copy.16 = f32[12,64,7,128]{3,0,2,1:T(8,128)} copy(f32[12,64,7,128]{3,2,1,0:T(8,128)} %bitcast.12) | data formatting | bytes 5505024 | tf_op jit(solution)/shard_map/reshape | solution.py:114
  19.6 6.6 %gather_fusion.1 = f32[768,7,128]{2,1,0:T(8,128)} fusion(f32[4,65,7,128]{3,2,1,0:T(8,128)S(1)} %concatenate.15, s32[768]{0:T(1024)S(1)} %reshape.229), kind=kCustom, calls=%fused_computation.1 | custom fusion | bytes 5511168 | tf_op jit(solution)/shard_map/gather | solution.py:114
  26.2 3.7 %copy.17 = f32[12,64,7,128]{3,0,2,1:T(8,128)S(1)} copy(f32[12,64,7,128]{3,2,1,0:T(8,128)} %bitcast.11) | data formatting | bytes 5505024 | tf_op jit(solution)/shard_map/reshape | solution.py:114
  29.9 3.0 %pad_maximum_fusion = f32[24,64,7,128]{3,0,2,1:T(8,128)} fusion(f32[12,64,7,128]{3,0,2,1:T(8,128)S(1)} %copy.17, f32[12,64,7,128]{3,0,2,1:T(8,128)S(1)} %copy-done), kind=kLoop, calls=%fused_computation.2 | loop fusion | flops 1376256 | bytes 11010048 | tf_op jit(solution)/shard_map/concatenate | solution.py:24
  32.9 11.1 %all-to-all-start = ((f32[24,64,7,128]{3,0,2,1:T(8,128)}), f32[24,64,7,128]{3,0,2,1:T(8,128)}, u32[]{:S(2)}, u32[]{:S(2)}) async-start(f32[24,64,7,128]{3,0,2,1:T(8,128)} %pad_maximum_fusion), calls=%async_computation | async-start | bytes 11010048 | tf_op jit(solution)/shard_map/all_to_all | solution.py:27
  44.1 0.1 fusion.9
  44.2 7.0 %multiply_reduce_fusion.1 = (f32[4,64]{1,0:T(4,128)S(1)}, f32[4,64]{1,0:T(4,128)S(1)}) fusion(f32[4,64,7,128]{3,2,1,0:T(8,128)S(1)} %copy-done.1, s32[4,64,7]{2,1,0:T(8,128)S(1)} %get-tuple-element.10, s32[4,64,7]{2,1,0:T(8,128)S(1)} %get-tuple-element.9, f32[4,64,7,128]{3,2,1,0:T(8,128)S(1)} %reshape.221), kind=kLoop, calls=%fused_computation.8 | loop fusion | flops 3669504 | bytes 1851392 | tf_op jit(solution)/shard_map/reduce_sum | solution.py:106
  51.2 0.1 mul.152
  51.3 0.1 mul.155
  51.4 0.1 fusion.8
  51.5 0.1 multiply_reduce_fusion.2
  51.7 0.1 broadcast_multiply_fusion
  51.7 21.1 %psum.35 = f32[4,2,256]{2,1,0:T(2,128)S(1)} all-reduce(f32[4,2,256]{2,1,0:T(2,128)S(1)} %broadcast_multiply_fusion), channel_id=1, replica_groups=mesh['dp_0'=4,'dp_1'=4,'dp_2'=4,'expert_0'=2,'expert_1'=2] {'dp_0'}, use_global_device_ids=true, to_apply=%region_6.7 | all-reduce | flops 2048 | bytes 16384 | tf_op jit(solution)/shard_map/psum | solution.py:36
  72.9 92.0 %psum.36 = f32[4,2,256]{2,1,0:T(2,128)S(1)} all-reduce(f32[4,2,256]{2,1,0:T(2,128)S(1)} %psum.35), channel_id=1, replica_groups=mesh['dp_0'=4,'dp_1'=4,'dp_2'=4,'expert_0'=2,'expert_1'=2] {'dp_1'}, use_global_device_ids=true, to_apply=%region_7.8 | all-reduce | flops 2048 | bytes 16384 | tf_op jit(solution)/shard_map/psum | solution.py:36
  164.9 8.5 %psum.37 = f32[4,2,256]{2,1,0:T(2,128)S(1)} all-reduce(f32[4,2,256]{2,1,0:T(2,128)S(1)} %psum.36), channel_id=1, replica_groups=mesh['dp_0'=4,'dp_1'=4,'dp_2'=4,'expert_0'=2,'expert_1'=2] {'dp_2'}, use_global_device_ids=true, to_apply=%region_8.9 | all-reduce | flops 2048 | bytes 16384 | tf_op jit(solution)/shard_map/psum | solution.py:36
  173.4 7.8 %psum.38 = f32[4,2,256]{2,1,0:T(2,128)S(1)} all-reduce(f32[4,2,256]{2,1,0:T(2,128)S(1)} %psum.37), channel_id=1, replica_groups=mesh['dp_0'=4,'dp_1'=4,'dp_2'=4,'expert_0'=2,'expert_1'=2] {'expert_0'}, use_global_device_ids=true, to_apply=%region_9.10 | all-reduce | flops 2048 | bytes 16384 | tf_op jit(solution)/shard_map/psum | solution.py:36
  181.2 8.5 %psum.39 = f32[4,2,256]{2,1,0:T(2,128)} all-reduce(f32[4,2,256]{2,1,0:T(2,128)S(1)} %psum.38), channel_id=1, replica_groups=mesh['dp_0'=4,'dp_1'=4,'dp_2'=4,'expert_0'=2,'expert_1'=2] {'expert_1'}, use_global_device_ids=true, to_apply=%region_10.11 | all-reduce | flops 2048 | bytes 16384 | tf_op jit(solution)/shard_map/psum | solution.py:36
  189.7 6.8 %fusion.17 = (f32[12,64,7,128]{3,0,2,1:T(8,128)}, f32[12,64,7,128]{3,0,2,1:T(8,128)}) fusion(f32[24,64,7,128]{3,0,2,1:T(8,128)} %all-to-all-done), kind=kLoop, calls=%fused_computation.47 | loop fusion | bytes 11010048 | tf_op jit(solution)/shard_map/split | solution.py:26
  196.5 6.0 %reshape.244 = f32[1,4,3,448,128]{4,2,1,3,0:T(4,128)} reshape(f32[12,64,7,128]{3,0,2,1:T(8,128)} %get-tuple-element.7) | data formatting | bytes 5505024 | tf_op jit(solution)/shard_map/reshape;reshape | solution.py:130
  202.5 4.5 %copy.21 = f32[1,4,3,448,128]{4,3,2,1,0:T(8,128)} copy(f32[1,4,3,448,128]{4,2,1,3,0:T(4,128)} %reshape.244) | data formatting | bytes 5505024 | tf_op jit(solution)/shard_map/reshape;reshape | solution.py:130
  206.9 6.0 %reshape.243 = f32[1,4,3,448,128]{4,2,1,3,0:T(4,128)} reshape(f32[12,64,7,128]{3,0,2,1:T(8,128)} %get-tuple-element.8) | data formatting | bytes 5505024 | tf_op jit(solution)/shard_map/reshape;reshape | solution.py:130
  213.0 4.5 %copy.20 = f32[1,4,3,448,128]{4,3,2,1,0:T(8,128)} copy(f32[1,4,3,448,128]{4,2,1,3,0:T(4,128)} %reshape.243) | data formatting | bytes 5505024 | tf_op jit(solution)/shard_map/reshape;reshape | solution.py:130
  (18 shorter events, 0.1 us)
Async XLA Ops:
  0.6 4.5 %copy-start.2 = (f32[1,112,2048]{2,1,0:T(8,128)S(1)}, f32[1,112,2048]{2,1,0:T(8,128)}, u32[]{:S(2)}) copy-start(f32[1,112,2048]{2,1,0:T(8,128)} %param.5) | copy-start | bytes 2752516
  26.2 3.7 %copy-start = (f32[12,64,7,128]{3,0,2,1:T(8,128)S(1)}, f32[12,64,7,128]{3,0,2,1:T(8,128)}, u32[]{:S(2)}) copy-start(f32[12,64,7,128]{3,0,2,1:T(8,128)} %copy.16) | copy-start | bytes 8257540
  32.9 11.3 %copy-start.1 = (f32[4,64,7,128]{3,2,1,0:T(8,128)S(1)}, f32[4,64,7,128]{3,2,1,0:T(8,128)}, u32[]{:S(2)}) copy-start(f32[4,64,7,128]{3,2,1,0:T(8,128)} %reshape.219) | copy-start | bytes 2752516
  32.9 18.5 %copy-start.3 = (s32[256]{0:T(256)S(1)}, s32[256]{0:T(256)}, u32[]{:S(2)}) copy-start(s32[256]{0:T(256)} %param.9) | copy-start | bytes 3076
  32.9 156.7 %all-to-all-start = ((f32[24,64,7,128]{3,0,2,1:T(8,128)}), f32[24,64,7,128]{3,0,2,1:T(8,128)}, u32[]{:S(2)}, u32[]{:S(2)}) async-start(f32[24,64,7,128]{3,0,2,1:T(8,128)} %pad_maximum_fusion), calls=%async_computation | async-start | bytes 11010048 | tf_op jit(solution)/shard_map/all_to_all | solution.py:27
where the time goes:
time: 218 us; the launch traced here: 217 us
  blocking collectives  138 us (63%)
  local copies, waits for them, and re-layouts  53 us (24%)
  other arithmetic  14.6 us (7%)
  starting transfers between devices  11.1 us (5%)
    psum x5, blocking collectives, one_axis_at_a_time(): array = lax.psum(array, axis)  138 us
    gather x2, local copies, waits for them, and re-layouts, shards(): source[round_ids, table]  13.2 us
    all_to_all x1, starting transfers between devices, sent_together(): lax.all_to_all(both, axis, split_axis=split_dim, concat_axis=concat_dim,...  11.1 us
    another operation x2, local copies, waits for them, and re-layouts, shards(): saved_update.reshape(shape_out)  10.5 us
    another operation x2, local copies, waits for them, and re-layouts, shards(): saved_master.reshape(shape_out)  10.5 us
    reshape x2, local copies, waits for them, and re-layouts, shards(): source[round_ids, table]  9.03 us
    reduce_sum x1, other arithmetic, shards(): jnp.sum(master_lines * weights, axis=(2, 3)).reshape(round_count * dp_count)  6.96 us
    split x1, local copies, waits for them, and re-layouts, sent_together(): jnp.split(lax.all_to_all(both, axis, split_axis=split_dim, concat_axis=co...  6.82 us
  transfers between devices with their start and end apart: 1, of which 0 were waited for; matrix products, arithmetic and copies ran while one was open for 3% of the time, Pallas kernels for 0%

commit v1 on v0

--- a/solution.py
+++ b/solution.py
@@ -33,7 +33,7 @@
 
 def one_axis_at_a_time(array, axes):
     for axis in axes:
-        array = lax.psum(array, axis)
+        array = jnp.sum(lax.all_gather(array, axis), axis=0)
     return array
 
 

time: 218 us -> 225 us (1.032); the launches traced: 217 us -> 221 us
  blocking collectives: 138 us -> 141 us
    all_gather x0 -> x5, blocking collectives: none -> 141 us  [one_axis_at_a_time(): array = jnp.sum(lax.all_gather(array, axis), axis=0)]
    psum x5 -> x0, blocking collectives: 138 us -> none  [one_axis_at_a_time(): array = lax.psum(array, axis)]
  transfers between devices with their start and end apart: 1 -> 1, of which waited for: 0 -> 0; matrix products, arithmetic and copies ran while one was open for 3% -> 4% of each run, Pallas kernels for 0% -> 0%
where the time goes in v1:
time: 225 us; the launch traced here: 221 us
  blocking collectives  141 us (63%)
  local copies, waits for them, and re-layouts  53 us (24%)
  other arithmetic  15.3 us (7%)
  starting transfers between devices  11.1 us (5%)
    all_gather x5, blocking collectives, one_axis_at_a_time(): array = jnp.sum(lax.all_gather(array, axis), axis=0)  141 us
    gather x2, local copies, waits for them, and re-layouts, shards(): source[round_ids, table]  13.2 us
    all_to_all x1, starting transfers between devices, sent_together(): lax.all_to_all(both, axis, split_axis=split_dim, concat_axis=concat_dim,...  11.1 us
    another operation x2, local copies, waits for them, and re-layouts, shards(): saved_update.reshape(shape_out)  10.5 us
    another operation x2, local copies, waits for them, and re-layouts, shards(): saved_master.reshape(shape_out)  10.5 us
    reshape x2, local copies, waits for them, and re-layouts, shards(): source[round_ids, table]  9.03 us
    reduce_sum x1, other arithmetic, shards(): jnp.sum(master_lines * weights, axis=(2, 3)).reshape(round_count * dp_count)  6.96 us
    split x1, local copies, waits for them, and re-layouts, sent_together(): jnp.split(lax.all_to_all(both, axis, split_axis=split_dim, concat_axis=co...  6.82 us
  transfers between devices with their start and end apart: 1, of which 0 were waited for; matrix products, arithmetic and copies ran while one was open for 4% of the time, Pallas kernels for 0%

profile of v1, /device:TPU:71, one launch (start us, length us, event | category | flops | bytes accessed | tf_op | source)
XLA Modules:
  0.0 220.8 jit_solution(14728814399680507617)
XLA Ops:
  0.7 0.8 iota_compare_fusion.1
  1.4 1.0 convert_reduce_fusion
  2.4 0.5 fusion.7
  3.0 0.1 reshape.232
  3.1 1.8 add_divide_fusion
  4.9 0.2 reshape.224
  5.1 1.2 reshape.222
  6.3 1.3 concatenate.13
  7.6 6.6 %gather_fusion = f32[768,7,128]{2,1,0:T(8,128)} fusion(f32[4,65,7,128]{3,2,1,0:T(8,128)S(1)} %concatenate.13, s32[768]{0:T(1024)S(1)} %reshape.232), kind=kCustom, calls=%fused_computation | custom fusion | bytes 5511168 | tf_op jit(solution)/shard_map/gather | solution.py:114
  14.3 5.3 %copy.22 = f32[12,64,7,128]{3,0,2,1:T(8,128)} copy(f32[12,64,7,128]{3,2,1,0:T(8,128)} %bitcast.16) | data formatting | bytes 5505024 | tf_op jit(solution)/shard_map/reshape | solution.py:114
  19.6 6.6 %gather_fusion.1 = f32[768,7,128]{2,1,0:T(8,128)} fusion(f32[4,65,7,128]{3,2,1,0:T(8,128)S(1)} %concatenate.15, s32[768]{0:T(1024)S(1)} %reshape.232), kind=kCustom, calls=%fused_computation.1 | custom fusion | bytes 5511168 | tf_op jit(solution)/shard_map/gather | solution.py:114
  26.2 3.7 %copy.23 = f32[12,64,7,128]{3,0,2,1:T(8,128)S(1)} copy(f32[12,64,7,128]{3,2,1,0:T(8,128)} %bitcast.15) | data formatting | bytes 5505024 | tf_op jit(solution)/shard_map/reshape | solution.py:114
  29.9 3.0 %pad_maximum_fusion = f32[24,64,7,128]{3,0,2,1:T(8,128)} fusion(f32[12,64,7,128]{3,0,2,1:T(8,128)S(1)} %copy.23, f32[12,64,7,128]{3,0,2,1:T(8,128)S(1)} %copy-done), kind=kLoop, calls=%fused_computation.2 | loop fusion | flops 1376256 | bytes 11010048 | tf_op jit(solution)/shard_map/concatenate | solution.py:24
  32.9 11.1 %all-to-all-start = ((f32[24,64,7,128]{3,0,2,1:T(8,128)}), f32[24,64,7,128]{3,0,2,1:T(8,128)}, u32[]{:S(2)}, u32[]{:S(2)}) async-start(f32[24,64,7,128]{3,0,2,1:T(8,128)} %pad_maximum_fusion), calls=%async_computation | async-start | bytes 11010048 | tf_op jit(solution)/shard_map/all_to_all | solution.py:27
  44.1 0.1 fusion.9
  44.2 7.0 %multiply_reduce_fusion.1 = (f32[4,64]{1,0:T(4,128)S(1)}, f32[4,64]{1,0:T(4,128)S(1)}) fusion(f32[4,64,7,128]{3,2,1,0:T(8,128)S(1)} %copy-done.1, s32[4,64,7]{2,1,0:T(8,128)S(1)} %get-tuple-element.10, s32[4,64,7]{2,1,0:T(8,128)S(1)} %get-tuple-element.9, f32[4,64,7,128]{3,2,1,0:T(8,128)S(1)} %reshape.224), kind=kLoop, calls=%fused_computation.8 | loop fusion | flops 3669504 | bytes 1851392 | tf_op jit(solution)/shard_map/reduce_sum | solution.py:106
  51.2 0.1 mul.159
  51.3 0.1 mul.162
  51.4 0.1 fusion.8
  51.5 0.1 multiply_reduce_fusion.2
  51.7 0.1 broadcast_multiply_fusion
  51.7 22.0 %all_gather.28 = f32[4,4,2,256]{3,1,2,0:T(4,128)S(1)} all-gather(f32[1,4,2,256]{3,1,2,0:T(4,128)S(1)} %broadcast_multiply_fusion), channel_id=1, replica_groups=mesh['dp_0'=4,'dp_1'=4,'dp_2'=4,'expert_0'=2,'expert_1'=2] {'dp_0'}, dimensions={0}, use_global_device_ids=true | all-gather | bytes 40960 | tf_op jit(solution)/shard_map/all_gather | solution.py:36
  73.7 92.1 %all-gather = f32[16,2,256]{2,1,0:T(2,128)S(1)} all-gather(f32[4,2,256]{2,1,0:T(2,128)S(1)} %copy.26), channel_id=2, replica_groups=mesh['dp_0'=4,'dp_1'=4,'dp_2'=4,'expert_0'=2,'expert_1'=2] {'dp_1'}, dimensions={0}, use_global_device_ids=true | all-gather | bytes 40960 | tf_op jit(solution)/shard_map/all_gather | solution.py:36
  165.8 11.5 %all-gather.1 = f32[16,2,256]{2,1,0:T(2,128)S(1)} all-gather(f32[4,2,256]{2,1,0:T(2,128)S(1)} %reduce_sum.106), channel_id=3, replica_groups=mesh['dp_0'=4,'dp_1'=4,'dp_2'=4,'expert_0'=2,'expert_1'=2] {'dp_2'}, dimensions={0}, use_global_device_ids=true | all-gather | bytes 40960 | tf_op jit(solution)/shard_map/all_gather | solution.py:36
  177.4 7.1 %all-gather.2 = f32[8,2,256]{2,1,0:T(2,128)S(1)} all-gather(f32[4,2,256]{2,1,0:T(2,128)S(1)} %reduce_sum.107), channel_id=4, replica_groups=mesh['dp_0'=4,'dp_1'=4,'dp_2'=4,'expert_0'=2,'expert_1'=2] {'expert_0'}, dimensions={0}, use_global_device_ids=true | all-gather | bytes 24576 | tf_op jit(solution)/shard_map/all_gather | solution.py:36
  184.5 7.9 %all-gather.3 = f32[8,2,256]{2,1,0:T(2,128)S(1)} all-gather(f32[4,2,256]{2,1,0:T(2,128)S(1)} %reduce_sum.108), channel_id=5, replica_groups=mesh['dp_0'=4,'dp_1'=4,'dp_2'=4,'expert_0'=2,'expert_1'=2] {'expert_1'}, dimensions={0}, use_global_device_ids=true | all-gather | bytes 24576 | tf_op jit(solution)/shard_map/all_gather | solution.py:36
  192.4 0.6 reduce_sum.109
  193.0 6.8 %fusion.17 = (f32[12,64,7,128]{3,0,2,1:T(8,128)}, f32[12,64,7,128]{3,0,2,1:T(8,128)}) fusion(f32[24,64,7,128]{3,0,2,1:T(8,128)} %all-to-all-done), kind=kLoop, calls=%fused_computation.47 | loop fusion | bytes 11010048 | tf_op jit(solution)/shard_map/split | solution.py:26
  199.8 6.0 %reshape.251 = f32[1,4,3,448,128]{4,2,1,3,0:T(4,128)} reshape(f32[12,64,7,128]{3,0,2,1:T(8,128)} %get-tuple-element.7) | data formatting | bytes 5505024 | tf_op jit(solution)/shard_map/reshape;reshape | solution.py:130
  205.8 4.5 %copy.28 = f32[1,4,3,448,128]{4,3,2,1,0:T(8,128)} copy(f32[1,4,3,448,128]{4,2,1,3,0:T(4,128)} %reshape.251) | data formatting | bytes 5505024 | tf_op jit(solution)/shard_map/reshape;reshape | solution.py:130
  210.3 6.0 %reshape.250 = f32[1,4,3,448,128]{4,2,1,3,0:T(4,128)} reshape(f32[12,64,7,128]{3,0,2,1:T(8,128)} %get-tuple-element.8) | data formatting | bytes 5505024 | tf_op jit(solution)/shard_map/reshape;reshape | solution.py:130
  216.3 4.5 %copy.27 = f32[1,4,3,448,128]{4,3,2,1,0:T(8,128)} copy(f32[1,4,3,448,128]{4,2,1,3,0:T(4,128)} %reshape.250) | data formatting | bytes 5505024 | tf_op jit(solution)/shard_map/reshape;reshape | solution.py:130
  (24 shorter events, 0.2 us)
Async XLA Ops:
  0.6 4.5 %copy-start.2 = (f32[1,112,2048]{2,1,0:T(8,128)S(1)}, f32[1,112,2048]{2,1,0:T(8,128)}, u32[]{:S(2)}) copy-start(f32[1,112,2048]{2,1,0:T(8,128)} %param.5) | copy-start | bytes 2752516
  26.2 3.7 %copy-start = (f32[12,64,7,128]{3,0,2,1:T(8,128)S(1)}, f32[12,64,7,128]{3,0,2,1:T(8,128)}, u32[]{:S(2)}) copy-start(f32[12,64,7,128]{3,0,2,1:T(8,128)} %copy.22) | copy-start | bytes 8257540
  32.9 11.3 %copy-start.1 = (f32[4,64,7,128]{3,2,1,0:T(8,128)S(1)}, f32[4,64,7,128]{3,2,1,0:T(8,128)}, u32[]{:S(2)}) copy-start(f32[4,64,7,128]{3,2,1,0:T(8,128)} %reshape.222) | copy-start | bytes 2752516
  32.9 18.5 %copy-start.3 = (s32[256]{0:T(256)S(1)}, s32[256]{0:T(256)}, u32[]{:S(2)}) copy-start(s32[256]{0:T(256)} %param.9) | copy-start | bytes 3076
  32.9 160.1 %all-to-all-start = ((f32[24,64,7,128]{3,0,2,1:T(8,128)}), f32[24,64,7,128]{3,0,2,1:T(8,128)}, u32[]{:S(2)}, u32[]{:S(2)}) async-start(f32[24,64,7,128]{3,0,2,1:T(8,128)} %pad_maximum_fusion), calls=%async_computation | async-start | bytes 11010048 | tf_op jit(solution)/shard_map/all_to_all | solution.py:27
